TPU v7x, 512 devices: a 4x2x32 block of a 4x8x32 slice. The times are simulated.
512 devices in a mesh: parts: 2 (over y), tok: 32 (over z), hid: 8 (over x, core).
Axes of the slice: x: 4, y: 2, z: 32, core: 2. Of those that a mesh axis runs over, the one named last changes fastest.
The devices are a block of a 4x8x32 slice.
Arguments:
- tokens: bfloat16 [49152, 8192], P(('parts', 'tok'), 'hid'), parts along dimension 0, may hold values from -6 to 6
- adapter_ids: int32 [49152, 1], P(('parts', 'tok')), parts along dimension 0, may hold values from 0 to 255; in each aligned block of 768 rows (0 to 767, 768 to 1535, ...) at most 9 rows name the same one
- value_weight: bfloat16 [8192, 1024], P('hid'), may hold values from -0.0625 to 0.0625
- adapter_down: bfloat16 [256, 16, 8192], P('tok', None, 'hid'), may hold values from -0.0625 to 0.0625
- adapter_up: bfloat16 [256, 16, 1024], P('tok', None, 'hid'), may hold values from -1.5 to 1.5
Outputs:
- value_out: bfloat16 [49152, 1024], P(('parts', 'tok'), 'hid'), parts along dimension 0
There are 2 independent parts, one for each index of `parts`. A program takes and returns all parts, laid end to end along the dimension named above; an argument that names none is the same for every part. Nothing has to cross between parts.
Inputs may be any that keep to these rules, and one draw needn't show every extreme that they name: `adapter_ids`: among the 768 tokens of one index of tok, each adapter id appears at most 9 times; in some of these aligned blocks one id appears exactly 9 times.
All inputs are finite; a program needn't handle non-finite values.
Results may differ from a plain program's by a relative error of at most 0.0048.
Values may be sent and summed in bfloat16 or wider, within the bound.
No kernel may reach another device: no remote copies, remote signals or barrier semaphores. Data moves between devices by JAX's collectives and lax.ppermute only.
A program may use at most 128 MiB of HBM per device.

v0:
```python
import jax
import jax.numpy as jnp
from jax import lax
from jax.sharding import PartitionSpec as P


def split_up(array, dim, size):
    dims = array.shape
    blocks = array.reshape(*dims[:dim], size, dims[dim] // size, *dims[dim + 1 :])
    return jnp.moveaxis(blocks, dim, 0)


def sum_at_owner(array, axis, dim):
    size = lax.axis_size(axis)
    blocks = lax.all_to_all(split_up(array, dim, size), axis, 0, 0, tiled=True)
    return jnp.sum(blocks, axis=0)


def from_everyone(array, axis):
    size = lax.axis_size(axis)
    return lax.all_to_all(
        jnp.broadcast_to(array[None], (size, *array.shape)), axis, 0, 0, tiled=True
    )


def taken_together(array, axis):
    everything = from_everyone(array, axis)
    return jnp.sum(everything, axis=0)


def per_device(tokens, adapter_ids, value_weight, adapter_down, adapter_up):
    tok_rows, d_local = tokens.shape
    n_tok = lax.axis_size("tok")
    adp_dev = adapter_down.shape[0]
    low_rank = adapter_down.shape[1]
    kv_local = adapter_up.shape[2]
    adapters_all = adp_dev * n_tok
    capacity = max(2, 3 * tok_rows // adapters_all)
    token_ids = adapter_ids[:, 0]
    matches = token_ids[:, None] == token_ids[None, :]
    before = lax.broadcasted_iota(jnp.int32, (tok_rows, tok_rows), 0) > lax.broadcasted_iota(
        jnp.int32, (tok_rows, tok_rows), 1
    )
    position = jnp.sum((matches & before).astype(jnp.int32), axis=1)
    slot_index = token_ids * capacity + position
    slot_rows = (
        jnp.zeros((adapters_all * capacity, d_local), jnp.bfloat16).at[slot_index].set(tokens)
    )
    base_sums = sum_at_owner(
        lax.dot_general(
            value_weight, tokens, (((0,), (1,)), ((), ())), preferred_element_type=jnp.float32
        ),
        "hid",
        0,
    )
    weights_piece = lax.all_gather(adapter_down, "tok", axis=0, tiled=True)
    piece_count = weights_piece.shape[0]
    slot_block = slot_rows
    slot_block = slot_block.reshape(piece_count, capacity, d_local)
    partial_piece = jnp.einsum(
        "acn,arn->rac", slot_block, weights_piece, preferred_element_type=jnp.float32
    )
    partial_piece = partial_piece.reshape(low_rank, piece_count * capacity)
    low_rows = taken_together(partial_piece, "hid").astype(jnp.bfloat16)
    weights_piece = lax.all_gather(adapter_up, "tok", axis=0, tiled=True)
    piece_count = weights_piece.shape[0]
    low_block = low_rows
    low_block = low_block.reshape(low_rank, piece_count, capacity)
    expanded = jnp.einsum(
        "rac,ark->ack", low_block, weights_piece, preferred_element_type=jnp.float32
    )
    delta_slots = expanded.astype(jnp.bfloat16).reshape(piece_count * capacity, kv_local)
    delta_rows = delta_slots[slot_index]
    return (base_sums.T + delta_rows.astype(jnp.float32)).astype(jnp.bfloat16)


def solution(mesh):
    in_specs = (
        P(("parts", "tok"), "hid"),
        P(("parts", "tok"), None),
        P("hid", None),
        P("tok", None, "hid"),
        P("tok", None, "hid"),
    )
    out_specs = P(("parts", "tok"), "hid")
    return jax.shard_map(
        per_device, mesh=mesh, in_specs=in_specs, out_specs=out_specs, check_vma=False
    )
```

profile of v0, /device:TPU:34, one launch (start us, length us, event | category | flops | bytes accessed | tf_op | source)
XLA Modules:
  0.0 326.7 jit_solution(3771678501328643347)
XLA Ops:
  6.6 0.7 all-gather.3.cloned.1.call-update
  7.3 0.8 copy-done
  8.1 5.0 %fusion.6 = f32[1024,768]{1,0:T(8,128)} fusion(bf16[1024,1024]{1,0:T(8,128)(2,1)S(1)} %copy-done, bf16[768,1024]{1,0:T(8,128)(2,1)} %param.5), kind=kOutput, calls=%fused_computation.15 | convolution fusion | flops 1610612736 | bytes 6815744 | tf_op jit(solution)/shard_map/dot_general | solution.py:50
  13.1 44.9 %all-to-all-start = ((f32[8,128,768]{2,1,0:T(8,128)}), f32[8,128,768]{2,1,0:T(8,128)}, u32[]{:S(2)}, u32[]{:S(2)}) async-start(f32[8,128,768]{2,1,0:T(8,128)} %bitcast.14), calls=%async_computation | async-start | bytes 6291456 | tf_op jit(solution)/shard_map/all_to_all | solution.py:15
  58.1 0.8 all-gather.5.cloned.1.call-update
  58.9 0.4 convert_reduce_fusion
  59.2 9.3 %scatter_custom_fusion = bf16[2304,1024]{1,0:T(8,128)(2,1)} fusion(s32[768]{0:T(1024)S(1)} %fusion.5, bf16[768,1024]{1,0:T(8,128)(2,1)} %param.5, bf16[]{:T(256)} %constant.0.clone.1), kind=kCustom, calls=%fused_computation.4 | custom fusion | bytes 4719104 | tf_op jit(solution)/shard_map/scatter | solution.py:47
  68.6 9.5 %reshape.16 = bf16[256,9,1024]{2,1,0:T(8,128)(2,1)} reshape(bf16[2304,1024]{1,0:T(8,128)(2,1)} %scatter_custom_fusion) | data formatting | bytes 9437184 | tf_op jit(solution)/shard_map/reshape | solution.py:59
  78.1 107.0 %all-gather.3.cloned.1.call-done = bf16[256,16,1024]{2,1,0:T(8,128)(2,1)} async-done(((bf16[8,16,1024]{2,1,0:T(8,128)(2,1)}), bf16[256,16,1024]{2,1,0:T(8,128)(2,1)}) %all-gather.3.cloned.1.call-update) | async-done | bytes 8388624 | tf_op jit(solution)/shard_map/all_gather | solution.py:56
  185.0 10.5 %convolution_bitcast_fusion = f32[16,256,9]{0,2,1:T(8,128)} fusion(bf16[256,9,1024]{2,1,0:T(8,128)(2,1)} %reshape.16, bf16[256,16,1024]{2,1,0:T(8,128)(2,1)} %all-gather.3.cloned.1.call-done), kind=kOutput, calls=%fused_computation.7 | convolution fusion | flops 75497472 | bytes 13254656 | tf_op jit(solution)/shard_map/acn,arn->rac/dot_general | solution.py:60
  195.6 1.6 reshape.34
  197.2 0.3 copy.15
  197.5 1.1 broadcast_in_dim.14
  198.6 5.0 %all-to-all-start.1 = ((f32[8,16,2304]{2,1,0:T(8,128)}), f32[8,16,2304]{2,1,0:T(8,128)S(1)}, u32[]{:S(2)}, u32[]{:S(2)}) async-start(f32[8,16,2304]{2,1,0:T(8,128)} %broadcast_in_dim.14), calls=%async_computation.1 | async-start | bytes 2359296 | tf_op jit(solution)/shard_map/all_to_all | solution.py:21
  203.6 2.8 reduce_sum.29
  206.4 1.9 copy.12
  208.4 11.1 %all-to-all-done.1 = f32[8,16,2304]{2,1,0:T(8,128)S(1)} async-done(((f32[8,16,2304]{2,1,0:T(8,128)}), f32[8,16,2304]{2,1,0:T(8,128)S(1)}, u32[]{:S(2)}, u32[]{:S(2)}) %all-to-all-start.1) | async-done | bytes 1179680 | tf_op jit(solution)/shard_map/all_to_all | solution.py:21
  219.5 0.1 reduce_sum.32
  219.5 2.2 convert_element_type.21
  221.7 91.0 %all-gather.5.cloned.1.call-done = bf16[256,16,128]{2,1,0:T(8,128)(2,1)} async-done(((bf16[8,16,128]{2,1,0:T(8,128)(2,1)}), bf16[256,16,128]{2,1,0:T(8,128)(2,1)}) %all-gather.5.cloned.1.call-update) | async-done | bytes 1048592 | tf_op jit(solution)/shard_map/all_gather | solution.py:65
  312.7 3.0 convolution_convert_fusion
  315.7 1.5 reshape.17
  317.2 1.9 gather_fusion
  319.1 0.7 fusion.4
  (11 shorter events, 0.1 us)
Async XLA Ops:
  6.5 1.6 copy-start
  6.6 178.5 %all-gather.3.cloned.1.call-start = ((), (), s32[]{:S(2)}) async-start(), calls=%async_computation.2 | async-start | bytes 8650752 | tf_op jit(solution)/shard_map/all_gather | solution.py:56
  13.1 45.7 %copy-start.2 = (s32[768,1]{0,1:T(1,128)S(1)}, s32[768,1]{0,1:T(1,128)}, u32[]{:S(2)}) copy-start(s32[768,1]{0,1:T(1,128)} %param.6) | copy-start | bytes 9220
  13.1 184.4 %all-to-all-start = ((f32[8,128,768]{2,1,0:T(8,128)}), f32[8,128,768]{2,1,0:T(8,128)}, u32[]{:S(2)}, u32[]{:S(2)}) async-start(f32[8,128,768]{2,1,0:T(8,128)} %bitcast.14), calls=%async_computation | async-start | bytes 6291456 | tf_op jit(solution)/shard_map/all_to_all | solution.py:15
  58.1 254.7 %all-gather.5.cloned.1.call-start = ((), (), s32[]{:S(2)}) async-start(), calls=%async_computation.3 | async-start | bytes 1081344 | tf_op jit(solution)/shard_map/all_gather | solution.py:65
  198.6 20.9 %all-to-all-start.1 = ((f32[8,16,2304]{2,1,0:T(8,128)}), f32[8,16,2304]{2,1,0:T(8,128)S(1)}, u32[]{:S(2)}, u32[]{:S(2)}) async-start(f32[8,16,2304]{2,1,0:T(8,128)} %broadcast_in_dim.14), calls=%async_computation.1 | async-start | bytes 2359296 | tf_op jit(solution)/shard_map/all_to_all | solution.py:21
  315.7 3.4 %copy-start.1 = (f32[128,768]{0,1:T(8,128)S(1)}, f32[128,768]{0,1:T(8,128)}, u32[]{:S(2)}) copy-start(f32[128,768]{0,1:T(8,128)} %copy.12) | copy-start | bytes 1179652
Sparse Core Ops, SparseCore 0:
  9.4 175.5 all-gather.2
  187.1 125.5 all-gather.4
where the time goes:
time: 327 us
  waiting for transfers between devices  211 us (65%)
  starting transfers between devices  49.9 us (15%)
  local copies, waits for them, and re-layouts  30.2 us (9%)
  matrix products  18.6 us (6%)
  between operations  13.5 us (4%)
  other arithmetic  4.02 us (1%)
    all_gather x1, waiting for transfers between devices, per_device(): weights_piece = lax.all_gather(adapter_down, 'tok', axis=0, tiled=True)  107 us
    all_gather x1, waiting for transfers between devices, per_device(): weights_piece = lax.all_gather(adapter_up, 'tok', axis=0, tiled=True)  91 us
    all_to_all x1, starting transfers between devices, sum_at_owner(): blocks = lax.all_to_all(split_up(array, dim, size), axis, 0, 0, tiled=True)  44.9 us
    all_to_all x1, waiting for transfers between devices, from_everyone(): lax.all_to_all(jnp.broadcast_to(array[None], (size, *array.shape)), axis,...  11.1 us
    dot_general x1, matrix products, per_device(): jnp.einsum('acn,arn->rac', slot_block, weights_piece, preferred_element_t...  10.5 us
    reshape x1, local copies, waits for them, and re-layouts, per_device(): slot_block = slot_block.reshape(piece_count, capacity, d_local)  9.49 us
    scatter x1, local copies, waits for them, and re-layouts, per_device(): jnp.zeros((adapters_all * capacity, d_local), jnp.bfloat16).at[slot_index]  9.33 us
  transfers between devices with their start and end apart: 4, of which 3 were waited for; matrix products, arithmetic and copies ran while one was open for 14% of the time, Pallas kernels for 0%

commit v1 on v0

--- a/solution.py
+++ b/solution.py
@@ -2,6 +2,12 @@
 import jax.numpy as jnp
 from jax import lax
 from jax.sharding import PartitionSpec as P
+
+
+def tiled_gather(x, axis, dim):
+    peers = lax.axis_size(axis)
+    repeats = [peers if d == dim else 1 for d in range(x.ndim)]
+    return lax.all_to_all(jnp.tile(x, repeats), axis, split_axis=dim, concat_axis=dim, tiled=True)
 
 
 def split_up(array, dim, size):
@@ -53,7 +59,7 @@
         "hid",
         0,
     )
-    weights_piece = lax.all_gather(adapter_down, "tok", axis=0, tiled=True)
+    weights_piece = tiled_gather(adapter_down, "tok", 0)
     piece_count = weights_piece.shape[0]
     slot_block = slot_rows
     slot_block = slot_block.reshape(piece_count, capacity, d_local)

time: 327 us -> 938 us (2.87)
  waiting for transfers between devices: 211 us -> 810 us
    all_to_all x0 -> x1, waiting for transfers between devices: none -> 707 us  [tiled_gather(): lax.all_to_all(jnp.tile(x, repeats), axis, split_axis=dim, concat_axis=di...]
    all_gather x1 -> x0, waiting for transfers between devices: 107 us -> none  [per_device(): weights_piece = lax.all_gather(adapter_down, 'tok', axis=0, tiled=True)]
    all_to_all x0 -> x1, starting transfers between devices: none -> 45.8 us  [tiled_gather(): lax.all_to_all(jnp.tile(x, repeats), axis, split_axis=dim, concat_axis=di...]
    all_to_all x1, starting transfers between devices: 44.9 us -> 5.11 us  [sum_at_owner(): blocks = lax.all_to_all(split_up(array, dim, size), axis, 0, 0, tiled=True)]
  transfers between devices with their start and end apart: 4 -> 4, of which waited for: 3 -> 4; matrix products, arithmetic and copies ran while one was open for 14% -> 5% of each run, Pallas kernels for 0% -> 0%
where the time goes in v1:
time: 938 us; the launch traced here: 937 us
  waiting for transfers between devices  810 us (86%)
  starting transfers between devices  55.9 us (6%)
  local copies, waits for them, and re-layouts  34.7 us (4%)
  matrix products  18.6 us (2%)
  between operations  13.5 us (1%)
    all_to_all x1, waiting for transfers between devices, tiled_gather(): lax.all_to_all(jnp.tile(x, repeats), axis, split_axis=dim, concat_axis=di...  707 us
    all_gather x1, waiting for transfers between devices, per_device(): weights_piece = lax.all_gather(adapter_up, 'tok', axis=0, tiled=True)  86.7 us
    all_to_all x1, starting transfers between devices, tiled_gather(): lax.all_to_all(jnp.tile(x, repeats), axis, split_axis=dim, concat_axis=di...  45.8 us
  transfers between devices with their start and end apart: 4, of which 4 were waited for; matrix products, arithmetic and copies ran while one was open for 5% of the time, Pallas kernels for 0%

profile of v1, /device:TPU:34, one launch (start us, length us, event | category | flops | bytes accessed | tf_op | source)
XLA Modules:
  0.0 936.8 jit_solution(4342281210261695634)
XLA Ops:
  6.6 5.4 tile.4
  11.9 45.8 %all-to-all-start.1 = ((bf16[256,16,1024]{2,1,0:T(8,128)(2,1)}), bf16[256,16,1024]{2,1,0:T(8,128)(2,1)}, u32[]{:S(2)}, u32[]{:S(2)}) async-start(bf16[256,16,1024]{2,1,0:T(8,128)(2,1)} %bitcast.15), calls=%async_computation.1 | async-start | bytes 16777216 | tf_op jit(solution)/shard_map/all_to_all | solution.py:10
  57.7 5.0 fusion.6
  62.7 706.9 %all-to-all-done.1 = bf16[256,16,1024]{2,1,0:T(8,128)(2,1)} async-done(((bf16[256,16,1024]{2,1,0:T(8,128)(2,1)}), bf16[256,16,1024]{2,1,0:T(8,128)(2,1)}, u32[]{:S(2)}, u32[]{:S(2)}) %all-to-all-start.1) | async-done | bytes 8388640 | tf_op jit(solution)/shard_map/all_to_all | solution.py:10
  769.6 5.1 all-to-all-start
  774.7 0.7 all-gather.2.cloned.1.call-update
  775.5 0.4 convert_reduce_fusion
  775.9 9.3 scatter_custom_fusion
  785.2 9.5 %reshape.20 = bf16[256,9,1024]{2,1,0:T(8,128)(2,1)} reshape(bf16[2304,1024]{1,0:T(8,128)(2,1)} %scatter_custom_fusion) | data formatting | bytes 9437184 | tf_op jit(solution)/shard_map/reshape | solution.py:65
  794.7 10.5 %convolution_bitcast_fusion = f32[16,256,9]{0,2,1:T(8,128)} fusion(bf16[256,9,1024]{2,1,0:T(8,128)(2,1)} %reshape.20, bf16[256,16,1024]{2,1,0:T(8,128)(2,1)} %all-to-all-done.1), kind=kOutput, calls=%fused_computation.7 | convolution fusion | flops 75497472 | bytes 13254656 | tf_op jit(solution)/shard_map/acn,arn->rac/dot_general | solution.py:66
  805.2 1.6 reshape.38
  806.8 0.3 copy.15
  807.1 4.6 all-to-all-done
  811.8 1.1 broadcast_in_dim.14
  812.8 5.0 all-to-all-start.2
  817.8 2.8 reduce_sum.29
  820.7 1.9 copy.12
  822.6 11.2 %all-to-all-done.2 = f32[8,16,2304]{2,1,0:T(8,128)S(1)} async-done(((f32[8,16,2304]{2,1,0:T(8,128)}), f32[8,16,2304]{2,1,0:T(8,128)S(1)}, u32[]{:S(2)}, u32[]{:S(2)}) %all-to-all-start.2) | async-done | bytes 1179680 | tf_op jit(solution)/shard_map/all_to_all | solution.py:27
  833.8 2.2 convert_element_type.21
  836.1 86.7 %all-gather.2.cloned.1.call-done = bf16[256,16,128]{2,1,0:T(8,128)(2,1)} async-done(((bf16[8,16,128]{2,1,0:T(8,128)(2,1)}), bf16[256,16,128]{2,1,0:T(8,128)(2,1)}) %all-gather.2.cloned.1.call-update) | async-done | bytes 1048592 | tf_op jit(solution)/shard_map/all_gather | solution.py:71
  922.8 3.0 convolution_convert_fusion
  925.8 1.5 reshape.21
  927.3 1.9 gather_fusion
  929.2 0.7 fusion.4
  (11 shorter events, 0.1 us)
Async XLA Ops:
  6.5 51.2 %copy-start = (bf16[1024,1024]{1,0:T(8,128)(2,1)S(1)}, bf16[1024,1024]{1,0:T(8,128)(2,1)}, u32[]{:S(2)}) copy-start(bf16[1024,1024]{1,0:T(8,128)(2,1)} %param.7) | copy-start | bytes 6291460
  11.9 757.7 %all-to-all-start.1 = ((bf16[256,16,1024]{2,1,0:T(8,128)(2,1)}), bf16[256,16,1024]{2,1,0:T(8,128)(2,1)}, u32[]{:S(2)}, u32[]{:S(2)}) async-start(bf16[256,16,1024]{2,1,0:T(8,128)(2,1)} %bitcast.15), calls=%async_computation.1 | async-start | bytes 16777216 | tf_op jit(solution)/shard_map/all_to_all | solution.py:10
  769.6 5.9 copy-start.2
  769.6 42.2 %all-to-all-start = ((f32[8,128,768]{2,1,0:T(8,128)}), f32[8,128,768]{2,1,0:T(8,128)}, u32[]{:S(2)}, u32[]{:S(2)}) async-start(f32[8,128,768]{2,1,0:T(8,128)} %bitcast.16), calls=%async_computation | async-start | bytes 6291456 | tf_op jit(solution)/shard_map/all_to_all | solution.py:21
  774.7 148.1 %all-gather.2.cloned.1.call-start = ((), (), s32[]{:S(2)}) async-start(), calls=%async_computation.3 | async-start | bytes 1081344 | tf_op jit(solution)/shard_map/all_gather | solution.py:71
  812.8 20.9 %all-to-all-start.2 = ((f32[8,16,2304]{2,1,0:T(8,128)}), f32[8,16,2304]{2,1,0:T(8,128)S(1)}, u32[]{:S(2)}, u32[]{:S(2)}) async-start(f32[8,16,2304]{2,1,0:T(8,128)} %broadcast_in_dim.14), calls=%async_computation.2 | async-start | bytes 2359296 | tf_op jit(solution)/shard_map/all_to_all | solution.py:27
  925.8 3.4 copy-start.1
Sparse Core Ops, SparseCore 0:
  777.6 145.1 all-gather.1
